TPU v7x, 32 devices: a whole 2x2x4 slice. The times are simulated.
32 devices in a mesh: seq: 2 (over y), fsdp: 16 (over z, x, core).
Axes of the slice: x: 2, y: 2, z: 4, core: 2. Of those that a mesh axis runs over, the one named last changes fastest.
Arguments:
- tokens: bfloat16 [16, 1024, 1024], P('fsdp', 'seq'), may hold values from -6 to 6
- grad_out: bfloat16 [16, 1024, 1024], P('fsdp', 'seq'), may hold values from -6 to 6
- segments: int32 [16, 1024], P('fsdp'), may hold values from 0 to 1, as said below
- padding: int32 [16, 1024], P('fsdp'), may hold values from 0 to 1, as said below
- adapter_ids: int32 [16, 1], P('fsdp'), may hold values from 0 to 7
- norm1_gain: bfloat16 [1024], P('fsdp'), may hold values from 0.5 to 1.5
- norm1_bias: bfloat16 [1024], P('fsdp'), may hold values from -1.1953125 to 1.1953125
- w_qkv: bfloat16 [1024, 3072], P('fsdp'), may hold values from -0.1875 to 0.1875
- w_proj: bfloat16 [1024, 1024], P('fsdp'), may hold values from -3 to 3
- proj_bias: bfloat16 [1024], P('fsdp'), may hold values from -1.796875 to 1.796875
- norm2_gain: bfloat16 [1024], P('fsdp'), may hold values from 0.5 to 1.5
- norm2_bias: bfloat16 [1024], P('fsdp'), may hold values from -1.1953125 to 1.1953125
- w_fc1: bfloat16 [1024, 4096], P('fsdp'), may hold values from -0.1875 to 0.1875
- fc1_bias: bfloat16 [4096], P('fsdp'), may hold values from -3 to 3
- w_fc2: bfloat16 [4096, 1024], P('fsdp'), may hold values from -0.09375 to 0.09375
- fc2_bias: bfloat16 [1024], P('fsdp'), may hold values from -1.796875 to 1.796875
- qkv_down: bfloat16 [1024, 128], replicated, may hold values from -0.1875 to 0.1875
- qkv_up: bfloat16 [128, 3072], replicated, may hold values from -1.5 to 1.5
- proj_down: bfloat16 [1024, 128], replicated, may hold values from -3 to 3
- proj_up: bfloat16 [128, 1024], replicated, may hold values from -1.5 to 1.5
- fc1_down: bfloat16 [1024, 128], replicated, may hold values from -0.1875 to 0.1875
- fc1_up: bfloat16 [128, 4096], replicated, may hold values from -1.5 to 1.5
- fc2_down: bfloat16 [4096, 128], replicated, may hold values from -0.09375 to 0.09375
- fc2_up: bfloat16 [128, 1024], replicated, may hold values from -1.5 to 1.5
Outputs:
- output: bfloat16 [16, 1024, 1024], P('fsdp', 'seq')
- grad_tokens: float32 [16, 1024, 1024], P('fsdp', 'seq')
- grad_qkv_down: float32 [1024, 128], replicated
- grad_qkv_up: float32 [128, 3072], replicated
- grad_proj_down: float32 [1024, 128], replicated
- grad_proj_up: float32 [128, 1024], replicated
- grad_fc1_down: float32 [1024, 128], replicated
- grad_fc1_up: float32 [128, 4096], replicated
- grad_fc2_down: float32 [4096, 128], replicated
- grad_fc2_up: float32 [128, 1024], replicated
Inputs may be any that keep to these rules, and one draw needn't show every extreme that they name: `segments`: in each pack the tokens with padding 1 form 1 runs of exactly 577 tokens, in order; a token's segment number is the count of runs that begin at or before it, so run s has number s and padding takes the number of the run before it, or 0. `padding`: 1 exactly on the tokens of the runs. `adapter_ids`: entry s - 1 is the adapter of run s of the pack.
All inputs are finite; a program needn't handle non-finite values.
Results may differ from a plain program's by a relative error of at most 0.014.
The roundings to bfloat16 on the way count: a program that leaves them out, or rounds other values in their place, can miss the bound.
Values may be sent and summed in bfloat16 or wider, within the bound.
A program may use at most 192 MiB of HBM per device.

v0:
```python
from functools import partial
import jax
import jax.numpy as jnp
from jax import lax
from jax.sharding import PartitionSpec as P

HEAD_DIM = 64
IMG = 577
RANK = 16
QBLOCK = 512
norm_eps = 1e-06
masked_score = -1e30


def matmul(left_side, right_side):
    return jnp.dot(left_side, right_side, preferred_element_type=jnp.float32)


def matmul_nt(left_side, right_side):
    return jnp.einsum("tk,jk->tj", left_side, right_side, preferred_element_type=jnp.float32)


def matmul_tn(left_side, right_side):
    return jnp.einsum("ti,to->io", left_side, right_side, preferred_element_type=jnp.float32)


def layer_norm(values, norm_gain, norm_shift):
    centre = jnp.mean(values, axis=-1, keepdims=True)
    centred = values - centre
    spread = jnp.mean(centred * centred, axis=-1, keepdims=True)
    return centred * lax.rsqrt(spread + norm_eps) * norm_gain + norm_shift


def norm_backward(values, norm_gain, norm_shift, grad_in):

    def apply_norm(inputs):
        return layer_norm(inputs, norm_gain, norm_shift)

    unused, pullback = jax.vjp(apply_norm, values)
    return pullback(grad_in)[0]


def selection(seg_own, image_adapters, columns):
    images = jnp.arange(image_adapters.shape[0], dtype=jnp.int32)
    image_match = seg_own[:, None] - 1 == images[None, :]
    token_adapter = jnp.sum(jnp.where(image_match, image_adapters[None, :], 0), axis=1)
    present = jnp.any(image_match, axis=1)
    column = jnp.arange(columns, dtype=jnp.int32) // RANK
    chosen = (token_adapter[:, None] == column[None, :]) & present[:, None]
    return chosen.astype(jnp.float32)


def adapter_forward(inputs_b, weight, down_map, up_map, select):
    inner_term = (matmul(inputs_b, down_map) * select).astype(jnp.bfloat16)
    return (matmul(inputs_b, weight) + matmul(inner_term, up_map), inner_term)


def adapter_backward(inputs_b, inner_term, grad_in, weight, down_map, up_map, select):
    grad_up = matmul_tn(inner_term, grad_in)
    grad_inner = (matmul_nt(grad_in, up_map) * select).astype(jnp.bfloat16)
    grad_down = matmul_tn(inputs_b, grad_inner)
    grad_inputs = matmul_nt(grad_in, weight) + matmul_nt(grad_inner, down_map)
    return (grad_inputs, grad_down, grad_up)


def block_scores(query_block, key_heads, seg_block, seg_keys, keep_keys):
    score_scale = HEAD_DIM ** (-0.5)
    scores = (
        jnp.einsum("qhd,khd->hqk", query_block, key_heads, preferred_element_type=jnp.float32)
        * score_scale
    )
    allowed = (seg_block[:, None] == seg_keys[None, :]) & (keep_keys[None, :] == 1)
    return jnp.where(allowed[None, :, :], scores, masked_score)


def split_heads(head_rows):
    all_rows = head_rows.shape[0]
    local_heads = head_rows.shape[2] // HEAD_DIM
    query_heads = head_rows[:, 0].reshape(all_rows, local_heads, HEAD_DIM)
    key_heads = head_rows[:, 1].reshape(all_rows, local_heads, HEAD_DIM)
    value_heads = head_rows[:, 2].reshape(all_rows, local_heads, HEAD_DIM)
    return (query_heads, key_heads, value_heads)


def key_window(all_rows):
    return min(all_rows, (QBLOCK + 2 * IMG - 2 + 127) // 128 * 128)


def window_start(block_index, all_rows, window):
    first = block_index * QBLOCK - (IMG - 1)
    return jnp.clip(first, 0, all_rows - window)


def attention_forward(head_rows, seg_all, keep_all):
    all_rows = head_rows.shape[0]
    block_count = all_rows // QBLOCK
    window = key_window(all_rows)
    query_heads, key_heads, value_heads = split_heads(head_rows)
    local_heads = query_heads.shape[1]

    def one_block(block_parts):
        query_block, seg_block, keep_block, block_index = block_parts
        start = window_start(block_index, all_rows, window)
        keys_near = lax.dynamic_slice_in_dim(key_heads, start, window, 0)
        values_near = lax.dynamic_slice_in_dim(value_heads, start, window, 0)
        seg_near = lax.dynamic_slice_in_dim(seg_all, start, window, 0)
        keep_near = lax.dynamic_slice_in_dim(keep_all, start, window, 0)
        scores = block_scores(query_block, keys_near, seg_block, seg_near, keep_near)
        row_max = jnp.max(scores, axis=2, keepdims=True)
        weights = jnp.exp(scores - row_max)
        row_sum = jnp.sum(weights, axis=2, keepdims=True)
        probs_low = (weights / row_sum).astype(jnp.bfloat16)
        result = jnp.einsum(
            "hqk,khd->qhd", probs_low, values_near, preferred_element_type=jnp.float32
        )
        result = result * keep_block[:, None, None].astype(jnp.float32)
        return (result.astype(jnp.bfloat16), row_max, row_sum)

    block_ids = jnp.arange(block_count, dtype=jnp.int32)
    blocked = (
        query_heads.reshape(block_count, QBLOCK, local_heads, HEAD_DIM),
        seg_all.reshape(block_count, QBLOCK),
        keep_all.reshape(block_count, QBLOCK),
        block_ids,
    )
    results, block_max, block_sums = lax.map(one_block, blocked)
    return (results.reshape(all_rows, local_heads * HEAD_DIM), block_max, block_sums)


def attention_backward(head_rows, grad_rows, seg_all, keep_all, block_max, block_sums):
    all_rows = head_rows.shape[0]
    block_count = all_rows // QBLOCK
    window = key_window(all_rows)
    query_heads, key_heads, value_heads = split_heads(head_rows)
    local_heads = query_heads.shape[1]
    score_scale = HEAD_DIM ** (-0.5)

    def one_block(running, block_parts):
        grad_keys, grad_values = running
        query_block, seg_block, keep_block, grad_block, row_max, row_sum, block_index = block_parts
        start = window_start(block_index, all_rows, window)
        keys_near = lax.dynamic_slice_in_dim(key_heads, start, window, 0)
        values_near = lax.dynamic_slice_in_dim(value_heads, start, window, 0)
        seg_near = lax.dynamic_slice_in_dim(seg_all, start, window, 0)
        keep_near = lax.dynamic_slice_in_dim(keep_all, start, window, 0)
        scores = block_scores(query_block, keys_near, seg_block, seg_near, keep_near)
        probs = jnp.exp(scores - row_max) / row_sum
        grad_result = grad_block * keep_block[:, None, None].astype(jnp.bfloat16)
        values_term = jnp.einsum(
            "hqk,qhd->khd",
            probs.astype(jnp.bfloat16),
            grad_result,
            preferred_element_type=jnp.float32,
        )
        grad_probs = jnp.einsum(
            "qhd,khd->hqk", grad_result, values_near, preferred_element_type=jnp.float32
        )
        row_inner = jnp.sum(probs * grad_probs, axis=2, keepdims=True)
        grad_scores = (probs * (grad_probs - row_inner)).astype(jnp.bfloat16)
        grad_query = (
            jnp.einsum("hqk,khd->qhd", grad_scores, keys_near, preferred_element_type=jnp.float32)
            * score_scale
        )
        keys_term = (
            jnp.einsum("hqk,qhd->khd", grad_scores, query_block, preferred_element_type=jnp.float32)
            * score_scale
        )
        grad_keys = lax.dynamic_update_slice_in_dim(
            grad_keys, lax.dynamic_slice_in_dim(grad_keys, start, window, 0) + keys_term, start, 0
        )
        grad_values = lax.dynamic_update_slice_in_dim(
            grad_values,
            lax.dynamic_slice_in_dim(grad_values, start, window, 0) + values_term,
            start,
            0,
        )
        return ((grad_keys, grad_values), grad_query)

    zero_heads = jnp.zeros((all_rows, local_heads, HEAD_DIM), jnp.float32)
    block_ids = jnp.arange(block_count, dtype=jnp.int32)
    blocked = (
        query_heads.reshape(block_count, QBLOCK, local_heads, HEAD_DIM),
        seg_all.reshape(block_count, QBLOCK),
        keep_all.reshape(block_count, QBLOCK),
        grad_rows.reshape(block_count, QBLOCK, local_heads, HEAD_DIM),
        block_max,
        block_sums,
        block_ids,
    )
    (grad_keys, grad_values), grad_queries = lax.scan(one_block, (zero_heads, zero_heads), blocked)
    flat_width = local_heads * HEAD_DIM
    stacked = jnp.stack(
        [
            grad_queries.reshape(all_rows, flat_width),
            grad_keys.reshape(all_rows, flat_width),
            grad_values.reshape(all_rows, flat_width),
        ],
        axis=1,
    )
    return stacked.astype(jnp.bfloat16)


def per_device(
    tokens,
    grad_out,
    segments,
    padding,
    adapter_ids,
    norm1_gain,
    norm1_bias,
    w_qkv,
    w_proj,
    proj_bias,
    norm2_gain,
    norm2_bias,
    w_fc1,
    fc1_bias,
    w_fc2,
    fc2_bias,
    qkv_down,
    qkv_up,
    proj_down,
    proj_up,
    fc1_down,
    fc1_up,
    fc2_down,
    fc2_up,
):
    tok_rows = tokens.shape[1]
    feat_width = tokens.shape[2]
    inputs = tokens[0].astype(jnp.float32)
    seg_all = segments[0]
    keep_all = padding[0]
    offset = lax.axis_index("seq") * tok_rows
    seg_own = lax.dynamic_slice_in_dim(seg_all, offset, tok_rows)
    select = selection(seg_own, adapter_ids[0], qkv_down.shape[1])
    gain_one, shift_one, qkv_weight, proj_weight, proj_shift = (
        lax.all_gather(norm1_gain, "fsdp", axis=0, tiled=True),
        lax.all_gather(norm1_bias, "fsdp", axis=0, tiled=True),
        lax.all_gather(w_qkv, "fsdp", axis=0, tiled=True),
        lax.all_gather(w_proj, "fsdp", axis=0, tiled=True),
        lax.all_gather(proj_bias, "fsdp", axis=0, tiled=True),
    )
    gain_one = gain_one.astype(jnp.float32)
    shift_one = shift_one.astype(jnp.float32)
    normed_one = layer_norm(inputs, gain_one, shift_one).astype(jnp.bfloat16)
    qkv_main, inner_one = adapter_forward(normed_one, qkv_weight, qkv_down, qkv_up, select)
    qkv_low = qkv_main.astype(jnp.bfloat16).reshape(tok_rows, 3, feat_width)
    head_rows = lax.all_to_all(qkv_low, "seq", split_axis=2, concat_axis=0, tiled=True)
    attended_heads, block_max, block_sums = attention_forward(head_rows, seg_all, keep_all)
    attended = lax.all_to_all(attended_heads, "seq", split_axis=0, concat_axis=1, tiled=True)
    branch_one, inner_two = adapter_forward(attended, proj_weight, proj_down, proj_up, select)
    middle = inputs + (branch_one + proj_shift.astype(jnp.float32))
    gain_two, shift_two, fc1_weight, fc2_shift, fc2_weight, fc1_shift = (
        lax.all_gather(norm2_gain, "fsdp", axis=0, tiled=True),
        lax.all_gather(norm2_bias, "fsdp", axis=0, tiled=True),
        lax.all_gather(w_fc1, "fsdp", axis=0, tiled=True),
        lax.all_gather(fc2_bias, "fsdp", axis=0, tiled=True),
        lax.all_gather(w_fc2, "fsdp", axis=0, tiled=True),
        lax.all_gather(fc1_bias, "fsdp", axis=0, tiled=True),
    )
    gain_two = gain_two.astype(jnp.float32)
    shift_two = shift_two.astype(jnp.float32)
    normed_two = layer_norm(middle, gain_two, shift_two).astype(jnp.bfloat16)
    hidden_main, inner_three = adapter_forward(normed_two, fc1_weight, fc1_down, fc1_up, select)
    hidden = hidden_main + fc1_shift.astype(jnp.float32)
    active = jax.nn.gelu(hidden, approximate=False).astype(jnp.bfloat16)
    branch_two, inner_four = adapter_forward(active, fc2_weight, fc2_down, fc2_up, select)
    output = (middle + (branch_two + fc2_shift.astype(jnp.float32))).astype(jnp.bfloat16)
    fc1_back, fc2_back = (
        lax.all_gather(w_fc1, "fsdp", axis=0, tiled=True),
        lax.all_gather(w_fc2, "fsdp", axis=0, tiled=True),
    )
    grad_top = grad_out[0]
    grad_active, grad_fc2_down, grad_fc2_up = adapter_backward(
        active, inner_four, grad_top, fc2_back, fc2_down, fc2_up, select
    )
    unused, gelu_back = jax.vjp(partial(jax.nn.gelu, approximate=False), hidden)
    grad_hidden = gelu_back(grad_active)[0].astype(jnp.bfloat16)
    grad_normed_two, grad_fc1_down, grad_fc1_up = adapter_backward(
        normed_two, inner_three, grad_hidden, fc1_back, fc1_down, fc1_up, select
    )
    grad_middle = grad_top.astype(jnp.float32) + norm_backward(
        middle, gain_two, shift_two, grad_normed_two
    )
    qkv_back, proj_back = (
        lax.all_gather(w_qkv, "fsdp", axis=0, tiled=True),
        lax.all_gather(w_proj, "fsdp", axis=0, tiled=True),
    )
    grad_branch_one = grad_middle.astype(jnp.bfloat16)
    grad_attended, grad_proj_down, grad_proj_up = adapter_backward(
        attended, inner_two, grad_branch_one, proj_back, proj_down, proj_up, select
    )
    grad_head_rows = lax.all_to_all(
        grad_attended.astype(jnp.bfloat16), "seq", split_axis=1, concat_axis=0, tiled=True
    )
    grad_qkv_heads = attention_backward(
        head_rows, grad_head_rows, seg_all, keep_all, block_max, block_sums
    )
    grad_qkv = lax.all_to_all(
        grad_qkv_heads, "seq", split_axis=0, concat_axis=2, tiled=True
    ).reshape(tok_rows, 3 * feat_width)
    grad_normed_one, grad_qkv_down, grad_qkv_up = adapter_backward(
        normed_one, inner_one, grad_qkv, qkv_back, qkv_down, qkv_up, select
    )
    grad_tokens = grad_middle + norm_backward(inputs, gain_one, shift_one, grad_normed_one)
    summed = lax.psum(
        (
            grad_qkv_down,
            grad_qkv_up,
            grad_proj_down,
            grad_proj_up,
            grad_fc1_down,
            grad_fc1_up,
            grad_fc2_down,
            grad_fc2_up,
        ),
        ("seq", "fsdp"),
    )
    return (
        output[None],
        grad_tokens[None],
        summed[0],
        summed[1],
        summed[2],
        summed[3],
        summed[4],
        summed[5],
        summed[6],
        summed[7],
    )


def solution(mesh):
    return jax.shard_map(
        per_device,
        mesh=mesh,
        in_specs=(
            P("fsdp", "seq", None),
            P("fsdp", "seq", None),
            P("fsdp", None),
            P("fsdp", None),
            P("fsdp", None),
            P("fsdp"),
            P("fsdp"),
            P("fsdp", None),
            P("fsdp", None),
            P("fsdp"),
            P("fsdp"),
            P("fsdp"),
            P("fsdp", None),
            P("fsdp"),
            P("fsdp", None),
            P("fsdp"),
            P(),
            P(),
            P(),
            P(),
            P(),
            P(),
            P(),
            P(),
        ),
        out_specs=(
            P("fsdp", "seq", None),
            P("fsdp", "seq", None),
            P(),
            P(),
            P(),
            P(),
            P(),
            P(),
            P(),
            P(),
        ),
        check_vma=False,
    )
```

profile of v0, /device:TPU:0, one launch (start us, length us, event | category | flops | bytes accessed | tf_op | source)
XLA Modules:
  0.0 709.4 jit_solution(8467365100569532765)
XLA Ops:
  17.0 65.1 %all-reduce.7 = (bf16[1024]{0:T(1024)(128)(2,1)S(1)}, bf16[1024]{0:T(1024)(128)(2,1)S(1)}, bf16[1024]{0:T(1024)(128)(2,1)}, bf16[1024]{0:T(1024)(128)(2,1)}, bf1...) all-reduce(bf16[1024]{0:T(1024)(128)(2,1)S(1)} %dynamic-update-slice.1, ...), channel_id=1, replica_groups=mesh['seq'=2,'fsdp'=16] {'fsdp'}, use_global_device_ids=true, to_apply=%add.1 | all-reduce | flops 6144 | bytes 24576
  88.8 5.6 fusion.69
  101.7 6.6 copy.78
  108.4 5.7 all-to-all-start
  116.6 41.0 %all-to-all-done = bf16[512,3,1024]{0,1,2:T(4,128)(2,1)} async-done(((bf16[512,3,1024]{0,1,2:T(4,128)(2,1)}), bf16[512,3,1024]{0,1,2:T(4,128)(2,1)}, u32[]{:S(2)}, u32[]{:S(2)}) %all-to-all-start) | async-done | bytes 3145760 | tf_op jit(solution)/shard_map/all_to_all | solution.py:249
  157.6 4.7 copy.79
  162.3 4.8 copy.80
  179.7 30.4 %while.31 = (s32[]{:T(128)}, bf16[2,512,8,64]{1,3,2,0:T(8,128)(2,1)}, f32[2,8,512,1]{2,1,3,0:T(8,128)S(1)}, f32[2,8,512,1]{2,1,3,0:T(8,128)S(1)}, s32[2,512]{1,0...) while((s32[]{:T(128)}, ...), condition=%wide.region_5.6_spmd, body=%wide.region_2.5_spmd.sunk | while | flops 1125639680 | bytes 64133320 | solution.py:126
  188.5 5.4 fusion.169
  203.7 5.4 fusion.169
  215.2 18.0 %all-gather = bf16[16,1,256]{2,1,0:T(2,128)(2,1)S(1)} all-gather(bf16[1,1,256]{2,1,0:T(2,128)(2,1)S(1)} %reshape.288), channel_id=1, replica_groups=mesh['seq'=2,'fsdp'=16] {'fsdp'}, dimensions={0}, use_global_device_ids=true | all-gather | bytes 8704 | tf_op jit(solution)/shard_map/all_gather | solution.py:260
  245.5 7.7 %fusion.71 = f32[512,4096]{1,0:T(8,128)S(1)} fusion(bf16[512,1024]{1,0:T(8,128)(2,1)} %copy-done.26, bf16[1024,4096]{1,0:T(8,128)(2,1)} %all-gather.10.cloned.1.call-done), kind=kOutput, calls=%fused_computation.141 | convolution fusion | flops 4294967296 | bytes 17825792 | tf_op jit(solution)/shard_map/dot_general | solution.py:16
  253.2 21.1 %multiply_convert_fusion.1 = (bf16[512,4096]{1,0:T(8,128)(2,1)}, f32[512,4096]{1,0:T(8,128)}, f32[512,4096]{1,0:T(8,128)}) fusion(f32[4096]{0:T(1024)S(1)} %bitcast.250, f32[512,4096]{1,0:T(8,128)S(1)} %fusion.71, bf16[512,128]{1,0:T(8,128)(2,1)S(1)} %fusion.51, bf16[128,4096]{1,0:T(8,128)(2,1)S(1)} %copy-done), kind=kOutput, calls=%fused_computation.53 | convolution fusion | flops 677380096 | bytes 30556160 | tf_op jit(solution)/shard_map/dot_general | solution.py:16
  274.3 11.7 %fusion.60 = f32[512,4096]{1,0:T(8,128)} fusion(bf16[4096,1024]{1,0:T(8,128)(2,1)} %all-gather.12.cloned.1.call-done, bf16[1,512,1024]{2,1,0:T(8,128)(2,1)} %param.29), kind=kOutput, calls=%fused_computation.116 | convolution fusion | flops 4294967296 | bytes 17825792 | tf_op jit(solution)/shard_map/tk,jk->tj/dot_general | solution.py:20
  286.0 10.6 %add_convert_fusion = bf16[512,4096]{1,0:T(8,128)(2,1)S(1)} fusion(f32[512,4096]{1,0:T(8,128)} %get-tuple-element.444, f32[512,4096]{1,0:T(8,128)} %fusion.60, f32[512,4096]{1,0:T(8,128)} %get-tuple-element.458, bf16[512,128]{1,0:T(8,128)(2,1)S(1)} %copy-done.59, bf16[4096,128]{1,0:T(8,128)(2,1)S(1)} %copy-done.82), kind=kOutput, calls=%fused_computation.52 | convolution fusion | flops 568328192 | bytes 30539776 | tf_op jit(solution)/shard_map/tk,jk->tj/dot_general | solution.py:20
  319.9 9.6 %all-to-all-done.2 = bf16[512,2,512]{2,0,1:T(8,128)(2,1)} async-done(((bf16[512,2,512]{2,0,1:T(8,128)(2,1)}), bf16[512,2,512]{2,0,1:T(8,128)(2,1)}, u32[]{:S(2)}, u32[]{:S(2)}) %all-to-all-start.2) | async-done | bytes 1048608 | tf_op jit(solution)/shard_map/all_to_all | solution.py:294
  332.0 97.7 %while.32 = (s32[]{:T(128)}, f32[1024,8,64]{0,2,1:T(8,128)S(1)}, f32[1024,8,64]{0,2,1:T(8,128)}, bf16[2,512,8,64]{1,3,2,0:T(8,128)(2,1)}, bf16[2,512,8,64]{1,3,2...) while((s32[]{:T(128)}, f32[1024,8,64]{0,2,1:T(8,128)S(1)}, ...), condition=%wide.region_12.13_spmd.clone, body=%wide.region_10.12_spmd.clone.sunk | while | flops 2730751488 | bytes 175265136 | solution.py:190
  332.4 9.7 %fusion.177 = f32[8,512,1024]{2,1,0:T(8,128)} fusion(bf16[1024,8,64]{0,2,1:T(8,128)(2,1)} %get-tuple-element.712, bf16[2,512,8,64]{1,3,2,0:T(8,128)(2,1)} %get-tuple-element.710, s32[]{:T(128)S(6)} %copy.123, bf16[512]{0:T(512)(128)(2,1)S(1)} %convert_reduce_fusion.3), kind=kOutput, calls=%fused_computation.38.clone.1 | convolution fusion | flops 537133056 | bytes 18351108 | tf_op jit(solution)/shard_map/while/body/eval_jaxpr/qhd,khd->hqk/dot_general | solution.py:155
  342.1 14.8 %multiply_reduce_fusion.4 = (f32[8,512]{1,0:T(8,128)S(1)}, f32[8,512,1024]{2,1,0:T(8,128)}) fusion(f32[8,512,1024]{2,1,0:T(8,128)} %fusion.177, f32[8,512]{1,0:T(8,128)S(1)} %get-tuple-element.627, f32[8,512]{1,0:T(8,128)S(1)} %get-tuple-element.628, bf16[1024,8,64]{0,2,1:T(8,128)(2,1)S(1)} %get-tuple-element.707, ...), kind=kOutput, calls=%fused_computation.23.clone.1 | convolution fusion | flops 562032640 | bytes 35700740 | tf_op jit(solution)/shard_map/while/body/eval_jaxpr/qhd,khd->hqk/dot_general | solution.py:69
  357.0 11.5 %multiply_convert_fusion.3 = bf16[8,512,1024]{2,1,0:T(8,128)(2,1)S(1)} fusion(f32[8,512,1024]{2,1,0:T(8,128)} %get-tuple-element.629, f32[8,512,1024]{2,1,0:T(8,128)} %fusion.177, f32[8,512]{1,0:T(8,128)S(1)} %get-tuple-element.630), kind=kLoop, calls=%fused_computation.22.clone.1 | loop fusion | flops 12582912 | bytes 41959424 | tf_op jit(solution)/shard_map/while/body/eval_jaxpr/convert_element_type | solution.py:159
  368.5 7.8 %bitcast_add_fusion.5 = f32[1024,8,64]{0,2,1:T(8,128)S(1)} fusion(f32[1024,8,64]{0,2,1:T(8,128)S(1)} %copy-done.8, f32[8,512,1024]{2,1,0:T(8,128)} %get-tuple-element.629, pred[]{:T(512)S(6)} %compare.7, bf16[2,512,8,64]{1,3,2,0:T(8,128)(2,1)S(1)} %copy-done.13, s32[]{:T(128)S(6)} %copy.123, bf16[512]{0:T(512)(128)(2,1)S(1)} %convert_reduce_fusion.3), kind=kOutput, calls=%fused_computation.27.clone.1 | convolution fusion | flops 542375936 | bytes 21496836 | tf_op jit(solution)/shard_map/while/body/eval_jaxpr/hqk,qhd->khd/dot_general | solution.py:149
  381.3 9.7 %fusion.177 = f32[8,512,1024]{2,1,0:T(8,128)} fusion(bf16[1024,8,64]{0,2,1:T(8,128)(2,1)} %get-tuple-element.712, bf16[2,512,8,64]{1,3,2,0:T(8,128)(2,1)} %get-tuple-element.710, s32[]{:T(128)S(6)} %copy.123, bf16[512]{0:T(512)(128)(2,1)S(1)} %convert_reduce_fusion.3), kind=kOutput, calls=%fused_computation.38.clone.1 | convolution fusion | flops 537133056 | bytes 18351108 | tf_op jit(solution)/shard_map/while/body/eval_jaxpr/qhd,khd->hqk/dot_general | solution.py:155
  391.0 14.8 %multiply_reduce_fusion.4 = (f32[8,512]{1,0:T(8,128)S(1)}, f32[8,512,1024]{2,1,0:T(8,128)}) fusion(f32[8,512,1024]{2,1,0:T(8,128)} %fusion.177, f32[8,512]{1,0:T(8,128)S(1)} %get-tuple-element.627, f32[8,512]{1,0:T(8,128)S(1)} %get-tuple-element.628, bf16[1024,8,64]{0,2,1:T(8,128)(2,1)S(1)} %get-tuple-element.707, ...), kind=kOutput, calls=%fused_computation.23.clone.1 | convolution fusion | flops 562032640 | bytes 35700740 | tf_op jit(solution)/shard_map/while/body/eval_jaxpr/qhd,khd->hqk/dot_general | solution.py:69
  405.8 11.5 %multiply_convert_fusion.3 = bf16[8,512,1024]{2,1,0:T(8,128)(2,1)S(1)} fusion(f32[8,512,1024]{2,1,0:T(8,128)} %get-tuple-element.629, f32[8,512,1024]{2,1,0:T(8,128)} %fusion.177, f32[8,512]{1,0:T(8,128)S(1)} %get-tuple-element.630), kind=kLoop, calls=%fused_computation.22.clone.1 | loop fusion | flops 12582912 | bytes 41959424 | tf_op jit(solution)/shard_map/while/body/eval_jaxpr/convert_element_type | solution.py:159
  417.3 7.8 %bitcast_add_fusion.5 = f32[1024,8,64]{0,2,1:T(8,128)S(1)} fusion(f32[1024,8,64]{0,2,1:T(8,128)S(1)} %copy-done.8, f32[8,512,1024]{2,1,0:T(8,128)} %get-tuple-element.629, pred[]{:T(512)S(6)} %compare.7, bf16[2,512,8,64]{1,3,2,0:T(8,128)(2,1)S(1)} %copy-done.13, s32[]{:T(128)S(6)} %copy.123, bf16[512]{0:T(512)(128)(2,1)S(1)} %convert_reduce_fusion.3), kind=kOutput, calls=%fused_computation.27.clone.1 | convolution fusion | flops 542375936 | bytes 21496836 | tf_op jit(solution)/shard_map/while/body/eval_jaxpr/hqk,qhd->khd/dot_general | solution.py:149
  437.4 7.8 %copy.89 = bf16[1024,3,512]{2,1,0:T(4,128)(2,1)} copy(bf16[1024,3,512]{0,2,1:T(8,128)(2,1)} %pad_maximum_fusion) | data formatting | bytes 6291456 | tf_op jit(solution)/shard_map/stack | solution.py:192
  445.3 5.7 all-to-all-start.3
  462.5 35.9 %all-to-all-done.3 = bf16[1024,3,512]{2,1,0:T(4,128)(2,1)} async-done(((bf16[1024,3,512]{2,1,0:T(4,128)(2,1)}), bf16[1024,3,512]{2,1,0:T(4,128)(2,1)}, u32[]{:S(2)}, u32[]{:S(2)}) %all-to-all-start.3) | async-done | bytes 3145760 | tf_op jit(solution)/shard_map/all_to_all | solution.py:300
  503.0 4.8 copy.91
  514.5 8.4 %fusion.72 = f32[512,1024]{1,0:T(8,128)S(1)} fusion(bf16[512,4096]{1,0:T(8,128)(2,1)} %get-tuple-element.443, bf16[4096,1024]{1,0:T(8,128)(2,1)} %all-gather.12.cloned.1.call-done), kind=kOutput, calls=%fused_computation.142 | convolution fusion | flops 4294967296 | bytes 14680064 | tf_op jit(solution)/shard_map/dot_general | solution.py:16
  525.3 5.8 fusion.75
  535.0 156.9 %all-reduce.10.cloned.1.call-done = (f32[1024,128]{1,0:T(8,128)}, f32[128,3072]{1,0:T(8,128)}, f32[1024,128]{1,0:T(8,128)}, f32[128,1024]{1,0:T(8,128)}, f32[102...) async-done(((f32[1024,128]{1,0:T(8,128)}, f32[128,3072]{1,0:T(8,128)}, f32[1024,128]{1,0:T(8,128)}, f32[128,1024]{1,0:T(8,128)}, ...) | async-done | bytes 8388624 | tf_op jit(solution)/shard_map/psum | solution.py:307
  (339 shorter events, 156.6 us)
Async XLA Ops:
  7.2 246.0 %copy-start = (bf16[128,4096]{1,0:T(8,128)(2,1)S(1)}, bf16[128,4096]{1,0:T(8,128)(2,1)}, u32[]{:S(2)}) copy-start(bf16[128,4096]{1,0:T(8,128)(2,1)} %param.49) | copy-start | bytes 3145732
  7.2 81.1 %copy-start.55 = (bf16[1024,128]{1,0:T(8,128)(2,1)S(1)}, bf16[1024,128]{1,0:T(8,128)(2,1)}, u32[]{:S(2)}) copy-start(bf16[1024,128]{1,0:T(8,128)(2,1)} %param.44) | copy-start | bytes 786436
  7.2 81.6 %all-gather.6.cloned.1.call-start = ((), (), s32[]{:S(2)}) async-start(), calls=%async_computation.4 | async-start | bytes 6684672 | tf_op jit(solution)/shard_map/all_gather | solution.py:240
  7.9 229.5 %all-gather.8.cloned.1.call-start = ((), (), s32[]{:S(2)}) async-start(), calls=%async_computation.5 | async-start | bytes 2228224 | tf_op jit(solution)/shard_map/all_gather | solution.py:241
  8.7 236.8 %all-gather.10.cloned.1.call-start = ((), (), s32[]{:S(2)}) async-start(), calls=%async_computation.6 | async-start | bytes 8912896 | tf_op jit(solution)/shard_map/all_gather | solution.py:257
  108.4 49.2 %all-to-all-start = ((bf16[512,3,1024]{0,1,2:T(4,128)(2,1)}), bf16[512,3,1024]{0,1,2:T(4,128)(2,1)}, u32[]{:S(2)}, u32[]{:S(2)}) async-start(bf16[512,3,1024]{0,1,2:T(4,128)(2,1)} %copy.78), calls=%async_computation | async-start | bytes 8388608 | tf_op jit(solution)/shard_map/all_to_all | solution.py:249
  114.1 160.2 %all-gather.12.cloned.1.call-start = ((), (), s32[]{:S(2)}) async-start(), calls=%async_computation.7 | async-start | bytes 8912896 | tf_op jit(solution)/shard_map/all_gather | solution.py:259
  179.6 34.9 %copy-start.83 = (bf16[256]{0:T(256)(128)(2,1)S(1)}, bf16[256]{0:T(256)(128)(2,1)}, u32[]{:S(2)}) copy-start(bf16[256]{0:T(256)(128)(2,1)} %param.41) | copy-start | bytes 1540
  179.6 34.9 %copy-start.75 = (bf16[1024]{0:T(1024)(128)(2,1)S(1)}, bf16[1024]{0:T(1024)(128)(2,1)}, u32[]{:S(2)}) copy-start(bf16[1024]{0:T(1024)(128)(2,1)} %get-tuple-element.439) | copy-start | bytes 6148
  179.6 35.0 %copy-start.74 = (bf16[1024]{0:T(1024)(128)(2,1)S(1)}, bf16[1024]{0:T(1024)(128)(2,1)}, u32[]{:S(2)}) copy-start(bf16[1024]{0:T(1024)(128)(2,1)} %get-tuple-element.437) | copy-start | bytes 6148
  179.6 35.0 %copy-start.73 = (bf16[1024]{0:T(1024)(128)(2,1)S(1)}, bf16[1024]{0:T(1024)(128)(2,1)}, u32[]{:S(2)}) copy-start(bf16[1024]{0:T(1024)(128)(2,1)} %get-tuple-element.438) | copy-start | bytes 6148
  179.6 35.0 %copy-start.72 = (bf16[1024]{0:T(1024)(128)(2,1)S(1)}, bf16[1024]{0:T(1024)(128)(2,1)}, u32[]{:S(2)}) copy-start(bf16[1024]{0:T(1024)(128)(2,1)} %get-tuple-element.440) | copy-start | bytes 6148
  179.6 53.6 %copy-start.53 = (bf16[128,1024]{1,0:T(8,128)(2,1)S(1)}, bf16[128,1024]{1,0:T(8,128)(2,1)}, u32[]{:S(2)}) copy-start(bf16[128,1024]{1,0:T(8,128)(2,1)} %param.51) | copy-start | bytes 786436
  179.6 53.6 %copy-start.77 = (s32[512]{0:T(512)S(1)}, s32[512]{0:T(512)}, u32[]{:S(2)}) copy-start(s32[512]{0:T(512)} %copy-done.76) | copy-start | bytes 6148
  179.7 53.6 %copy-start.80 = (pred[512]{0:T(512)(128)(4,1)S(1)}, pred[512]{0:T(512)(128)(4,1)}, u32[]{:S(2)}) copy-start(pred[512]{0:T(512)(128)(4,1)} %copy-done.79) | copy-start | bytes 1540
  179.7 53.6 %copy-start.85 = (s32[128]{0:T(128)S(1)}, s32[128]{0:T(128)}, u32[]{:S(2)}) copy-start(s32[128]{0:T(128)} %copy-done.84) | copy-start | bytes 1540
  210.1 25.5 %all-to-all-start.1 = ((bf16[2,512,512]{1,2,0:T(8,128)(2,1)}), bf16[2,512,512]{1,2,0:T(8,128)(2,1)}, u32[]{:S(2)}, u32[]{:S(2)}) async-start(bf16[2,512,512]{1,2,0:T(8,128)(2,1)} %bitcast.244), calls=%async_computation.1 | async-start | bytes 2097152 | tf_op jit(solution)/shard_map/all_to_all | solution.py:251
  274.3 11.7 %copy-start.59 = (bf16[512,128]{1,0:T(8,128)(2,1)S(1)}, bf16[512,128]{1,0:T(8,128)(2,1)}, u32[]{:S(2)}) copy-start(bf16[512,128]{1,0:T(8,128)(2,1)} %fusion.53) | copy-start | bytes 393220
  274.3 11.7 %copy-start.82 = (bf16[4096,128]{1,0:T(8,128)(2,1)S(1)}, bf16[4096,128]{1,0:T(8,128)(2,1)}, u32[]{:S(2)}) copy-start(bf16[4096,128]{1,0:T(8,128)(2,1)} %param.50) | copy-start | bytes 3145732
  274.3 24.4 %slice-start = ((s8[8388608]{0:T(1024)(128)(4,1)}), s8[4194304]{0:T(1024)(128)(4,1)S(1)}, s32[]{:S(2)}) async-start(s8[8388608]{0:T(1024)(128)(4,1)} %bitcast.251), calls=%async_computation.9 | async-start | bytes 8388608
  286.0 12.7 %slice-start.1 = ((s8[8388608]{0:T(1024)(128)(4,1)}), s8[4194304]{0:T(1024)(128)(4,1)S(1)}, s32[]{:S(2)}) async-start(s8[8388608]{0:T(1024)(128)(4,1)} %bitcast.251), calls=%async_computation.10 | async-start | bytes 8388608
  310.4 21.5 %copy-start.3 = (bf16[1024,8,64]{0,2,1:T(8,128)(2,1)S(1)}, bf16[1024,8,64]{0,2,1:T(8,128)(2,1)}, u32[]{:S(2)}) copy-start(bf16[1024,8,64]{0,2,1:T(8,128)(2,1)} %copy-done.2) | copy-start | bytes 3145732
  310.4 19.1 %all-to-all-start.2 = ((bf16[512,2,512]{2,0,1:T(8,128)(2,1)}), bf16[512,2,512]{2,0,1:T(8,128)(2,1)}, u32[]{:S(2)}, u32[]{:S(2)}) async-start(bf16[512,2,512]{2,0,1:T(8,128)(2,1)} %bitcast.241), calls=%async_computation.2 | async-start | bytes 2097152 | tf_op jit(solution)/shard_map/all_to_all | solution.py:294
  332.4 9.7 %copy-start.14 = (bf16[2,512,8,64]{1,3,2,0:T(8,128)(2,1)S(1)}, bf16[2,512,8,64]{1,3,2,0:T(8,128)(2,1)}, u32[]{:S(2)}) copy-start(bf16[2,512,8,64]{1,3,2,0:T(8,128)(2,1)} %get-tuple-element.703) | copy-start | bytes 3145732 | tf_op jit(solution)/shard_map/while
  357.0 11.5 %copy-start.8 = (f32[1024,8,64]{0,2,1:T(8,128)S(1)}, f32[1024,8,64]{0,2,1:T(8,128)}, u32[]{:S(2)}) copy-start(f32[1024,8,64]{0,2,1:T(8,128)} %get-tuple-element.685) | copy-start | bytes 6291460 | tf_op jit(solution)/shard_map/while
  357.0 11.5 %copy-start.13 = (bf16[2,512,8,64]{1,3,2,0:T(8,128)(2,1)S(1)}, bf16[2,512,8,64]{1,3,2,0:T(8,128)(2,1)}, u32[]{:S(2)}) copy-start(bf16[2,512,8,64]{1,3,2,0:T(8,128)(2,1)} %get-tuple-element.710) | copy-start | bytes 3145732 | tf_op jit(solution)/shard_map/while
  381.3 9.7 %copy-start.14 = (bf16[2,512,8,64]{1,3,2,0:T(8,128)(2,1)S(1)}, bf16[2,512,8,64]{1,3,2,0:T(8,128)(2,1)}, u32[]{:S(2)}) copy-start(bf16[2,512,8,64]{1,3,2,0:T(8,128)(2,1)} %get-tuple-element.703) | copy-start | bytes 3145732 | tf_op jit(solution)/shard_map/while
  405.8 11.5 %copy-start.8 = (f32[1024,8,64]{0,2,1:T(8,128)S(1)}, f32[1024,8,64]{0,2,1:T(8,128)}, u32[]{:S(2)}) copy-start(f32[1024,8,64]{0,2,1:T(8,128)} %get-tuple-element.685) | copy-start | bytes 6291460 | tf_op jit(solution)/shard_map/while
  405.8 11.5 %copy-start.13 = (bf16[2,512,8,64]{1,3,2,0:T(8,128)(2,1)S(1)}, bf16[2,512,8,64]{1,3,2,0:T(8,128)(2,1)}, u32[]{:S(2)}) copy-start(bf16[2,512,8,64]{1,3,2,0:T(8,128)(2,1)} %get-tuple-element.710) | copy-start | bytes 3145732 | tf_op jit(solution)/shard_map/while
  445.3 53.1 %all-to-all-start.3 = ((bf16[1024,3,512]{2,1,0:T(4,128)(2,1)}), bf16[1024,3,512]{2,1,0:T(4,128)(2,1)}, u32[]{:S(2)}, u32[]{:S(2)}) async-start(bf16[1024,3,512]{2,1,0:T(4,128)(2,1)} %copy.89), calls=%async_computation.3 | async-start | bytes 8388608 | tf_op jit(solution)/shard_map/all_to_all | solution.py:300
  451.0 240.9 %all-reduce.10.cloned.1.call-start = ((), (), s32[]{:S(2)}) async-start(), calls=%async_computation.8 | async-start | bytes 16777216 | tf_op jit(solution)/shard_map/psum | solution.py:307
  514.5 8.4 %copy-start.7 = (f32[512,1024]{1,0:T(8,128)S(1)}, f32[512,1024]{1,0:T(8,128)}, u32[]{:S(2)}) copy-start(f32[512,1024]{1,0:T(8,128)} %copy-done.5) | copy-start | bytes 6291460
  (74 other events, 313.6 us)
Sparse Core Ops, SparseCore 0:
  10.3 64.6 all-gather.5
  77.2 40.2 all-gather.7
  119.6 73.0 all-gather.9
  194.7 72.8 all-gather.11
  514.6 177.2 all-reduce.9
where the time goes:
time: 718 us; the launch traced here: 709 us
  waiting for transfers between devices  246 us (34%)
  matrix products  210 us (29%)
  local copies, waits for them, and re-layouts  85.6 us (12%)
  blocking collectives  83.1 us (12%)
  other arithmetic  47.5 us (7%)
  starting transfers between devices  20.8 us (3%)
  between operations  16.7 us (2%)
    psum x1, waiting for transfers between devices, per_device(): lax.psum((grad_qkv_down, grad_qkv_up, grad_proj_down, grad_proj_up, grad_...  157 us
    unnamed x1, blocking collectives  65.1 us
    dot_general x12, matrix products, matmul(): return jnp.dot(left_side, right_side, preferred_element_type=jnp.float32)  58.6 us
    dot_general x12, matrix products, matmul_nt(): jnp.einsum('tk,jk->tj', left_side, right_side, preferred_element_type=jnp...  43 us
    all_to_all x1, waiting for transfers between devices, per_device(): lax.all_to_all(qkv_low, 'seq', split_axis=2, concat_axis=0, tiled=True)  41 us
    dot_general x4, matrix products, block_scores(): jnp.einsum('qhd,khd->hqk', query_block, key_heads, preferred_element_type...  37.9 us
    all_to_all x1, waiting for transfers between devices, per_device(): lax.all_to_all(grad_qkv_heads, 'seq', split_axis=0, concat_axis=2, tiled=...  35.9 us
    unnamed x185, local copies, waits for them, and re-layouts  25.5 us
  transfers between devices with their start and end apart: 9, of which 4 were waited for; matrix products, arithmetic and copies ran while one was open for 22% of the time, Pallas kernels for 0%

commit v1 on v0

--- a/solution.py
+++ b/solution.py
@@ -304,7 +304,7 @@
         normed_one, inner_one, grad_qkv, qkv_back, qkv_down, qkv_up, select
     )
     grad_tokens = grad_middle + norm_backward(inputs, gain_one, shift_one, grad_normed_one)
-    summed = lax.psum(
+    partial_2 = lax.psum(
         (
             grad_qkv_down,
             grad_qkv_up,
@@ -315,8 +315,9 @@
             grad_fc2_down,
             grad_fc2_up,
         ),
-        ("seq", "fsdp"),
-    )
+        "fsdp",
+    )
+    summed = lax.psum(partial_2, "seq")
     return (
         output[None],
         grad_tokens[None],

time: 718 us -> 909 us (1.27)
  waiting for transfers between devices: 246 us -> 437 us
    psum x0 -> x1, waiting for transfers between devices: none -> 180 us  [per_device(): summed = lax.psum(partial_2, 'seq')]
    psum x1, waiting for transfers between devices: 157 us -> 168 us  [per_device(): lax.psum((grad_qkv_down, grad_qkv_up, grad_proj_down, grad_proj_up, grad_...]
    unnamed x185 -> x183, local copies, waits for them, and re-layouts: 25.5 us -> 26.1 us
  transfers between devices with their start and end apart: 9 -> 10, of which waited for: 4 -> 5; matrix products, arithmetic and copies ran while one was open for 22% -> 18% of each run, Pallas kernels for 0% -> 0%
where the time goes in v1:
time: 909 us; the launch traced here: 901 us
  waiting for transfers between devices  437 us (48%)
  matrix products  210 us (23%)
  local copies, waits for them, and re-layouts  86.1 us (9%)
  blocking collectives  83.2 us (9%)
  other arithmetic  46.8 us (5%)
  starting transfers between devices  20.8 us (2%)
  between operations  17 us (2%)
    psum x1, waiting for transfers between devices, per_device(): summed = lax.psum(partial_2, 'seq')  180 us
    psum x1, waiting for transfers between devices, per_device(): lax.psum((grad_qkv_down, grad_qkv_up, grad_proj_down, grad_proj_up, grad_...  168 us
    unnamed x1, blocking collectives  65.1 us
    dot_general x12, matrix products, matmul(): return jnp.dot(left_side, right_side, preferred_element_type=jnp.float32)  58.8 us
    dot_general x12, matrix products, matmul_nt(): jnp.einsum('tk,jk->tj', left_side, right_side, preferred_element_type=jnp...  42.9 us
    all_to_all x1, waiting for transfers between devices, per_device(): lax.all_to_all(qkv_low, 'seq', split_axis=2, concat_axis=0, tiled=True)  41 us
    dot_general x4, matrix products, block_scores(): jnp.einsum('qhd,khd->hqk', query_block, key_heads, preferred_element_type...  37.8 us
    all_to_all x1, waiting for transfers between devices, per_device(): lax.all_to_all(grad_qkv_heads, 'seq', split_axis=0, concat_axis=2, tiled=...  36 us
  transfers between devices with their start and end apart: 10, of which 5 were waited for; matrix products, arithmetic and copies ran while one was open for 18% of the time, Pallas kernels for 0%

profile of v1, /device:TPU:0, one launch (start us, length us, event | category | flops | bytes accessed | tf_op | source)
XLA Modules:
  0.0 900.8 jit_solution(5816522163426195007)
XLA Ops:
  17.0 65.1 %all-reduce.8 = (bf16[1024]{0:T(1024)(128)(2,1)S(1)}, bf16[1024]{0:T(1024)(128)(2,1)S(1)}, bf16[1024]{0:T(1024)(128)(2,1)}, bf16[1024]{0:T(1024)(128)(2,1)}, bf1...) all-reduce(bf16[1024]{0:T(1024)(128)(2,1)S(1)} %dynamic-update-slice.1, ...), channel_id=1, replica_groups=mesh['seq'=2,'fsdp'=16] {'fsdp'}, use_global_device_ids=true, to_apply=%add.1 | all-reduce | flops 6144 | bytes 24576
  88.8 5.6 fusion.69
  101.7 6.6 copy.78
  108.3 5.7 all-to-all-start
  116.6 41.0 %all-to-all-done = bf16[512,3,1024]{0,1,2:T(4,128)(2,1)} async-done(((bf16[512,3,1024]{0,1,2:T(4,128)(2,1)}), bf16[512,3,1024]{0,1,2:T(4,128)(2,1)}, u32[]{:S(2)}, u32[]{:S(2)}) %all-to-all-start) | async-done | bytes 3145760 | tf_op jit(solution)/shard_map/all_to_all | solution.py:249
  162.2 4.7 copy.80
  179.6 30.4 %while.31 = (s32[]{:T(128)}, bf16[2,512,8,64]{1,3,2,0:T(8,128)(2,1)}, f32[2,8,512,1]{2,1,3,0:T(8,128)S(1)}, f32[2,8,512,1]{2,1,3,0:T(8,128)S(1)}, s32[2,512]{1,0...) while((s32[]{:T(128)}, ...), condition=%wide.region_5.6_spmd, body=%wide.region_2.5_spmd.sunk | while | flops 1125639680 | bytes 64133320 | solution.py:126
  188.5 5.4 fusion.169
  203.6 5.4 fusion.169
  214.5 18.1 %all-gather = bf16[16,1,256]{2,1,0:T(2,128)(2,1)S(1)} all-gather(bf16[1,1,256]{2,1,0:T(2,128)(2,1)S(1)} %reshape.288), channel_id=1, replica_groups=mesh['seq'=2,'fsdp'=16] {'fsdp'}, dimensions={0}, use_global_device_ids=true | all-gather | bytes 8704 | tf_op jit(solution)/shard_map/all_gather | solution.py:260
  244.9 7.7 fusion.71
  252.7 21.2 %multiply_convert_fusion.1 = (bf16[512,4096]{1,0:T(8,128)(2,1)}, f32[512,4096]{1,0:T(8,128)}, f32[512,4096]{1,0:T(8,128)}) fusion(f32[4096]{0:T(1024)S(1)} %bitcast.250, f32[512,4096]{1,0:T(8,128)S(1)} %fusion.71, bf16[512,128]{1,0:T(8,128)(2,1)S(1)} %fusion.51, bf16[128,4096]{1,0:T(8,128)(2,1)S(1)} %copy-done), kind=kOutput, calls=%fused_computation.53 | convolution fusion | flops 677380096 | bytes 30556160 | tf_op jit(solution)/shard_map/dot_general | solution.py:16
  273.9 11.7 %fusion.60 = f32[512,4096]{1,0:T(8,128)} fusion(bf16[4096,1024]{1,0:T(8,128)(2,1)} %all-gather.12.cloned.1.call-done, bf16[1,512,1024]{2,1,0:T(8,128)(2,1)} %param.29), kind=kOutput, calls=%fused_computation.116 | convolution fusion | flops 4294967296 | bytes 17825792 | tf_op jit(solution)/shard_map/tk,jk->tj/dot_general | solution.py:20
  285.6 10.6 %add_convert_fusion = bf16[512,4096]{1,0:T(8,128)(2,1)S(1)} fusion(f32[512,4096]{1,0:T(8,128)} %get-tuple-element.452, f32[512,4096]{1,0:T(8,128)} %fusion.60, f32[512,4096]{1,0:T(8,128)} %get-tuple-element.466, bf16[512,128]{1,0:T(8,128)(2,1)S(1)} %copy-done.59, bf16[4096,128]{1,0:T(8,128)(2,1)S(1)} %copy-done.81), kind=kOutput, calls=%fused_computation.52 | convolution fusion | flops 568328192 | bytes 30539776 | tf_op jit(solution)/shard_map/tk,jk->tj/dot_general | solution.py:20
  319.5 9.7 %all-to-all-done.2 = bf16[512,2,512]{2,0,1:T(8,128)(2,1)} async-done(((bf16[512,2,512]{2,0,1:T(8,128)(2,1)}), bf16[512,2,512]{2,0,1:T(8,128)(2,1)}, u32[]{:S(2)}, u32[]{:S(2)}) %all-to-all-start.2) | async-done | bytes 1048608 | tf_op jit(solution)/shard_map/all_to_all | solution.py:294
  331.6 97.7 %while.32 = (s32[]{:T(128)}, f32[1024,8,64]{0,2,1:T(8,128)S(1)}, f32[1024,8,64]{0,2,1:T(8,128)}, bf16[2,512,8,64]{1,3,2,0:T(8,128)(2,1)}, bf16[2,512,8,64]{1,3,2...) while((s32[]{:T(128)}, f32[1024,8,64]{0,2,1:T(8,128)S(1)}, ...), condition=%wide.region_12.13_spmd.clone, body=%wide.region_10.12_spmd.clone.sunk | while | flops 2730751488 | bytes 175265136 | solution.py:190
  332.1 9.7 %fusion.177 = f32[8,512,1024]{2,1,0:T(8,128)} fusion(bf16[1024,8,64]{0,2,1:T(8,128)(2,1)} %get-tuple-element.720, bf16[2,512,8,64]{1,3,2,0:T(8,128)(2,1)} %get-tuple-element.718, s32[]{:T(128)S(6)} %copy.123, bf16[512]{0:T(512)(128)(2,1)S(1)} %convert_reduce_fusion.3), kind=kOutput, calls=%fused_computation.38.clone.1 | convolution fusion | flops 537133056 | bytes 18351108 | tf_op jit(solution)/shard_map/while/body/eval_jaxpr/qhd,khd->hqk/dot_general | solution.py:155
  341.8 14.8 %multiply_reduce_fusion.4 = (f32[8,512]{1,0:T(8,128)S(1)}, f32[8,512,1024]{2,1,0:T(8,128)}) fusion(f32[8,512,1024]{2,1,0:T(8,128)} %fusion.177, f32[8,512]{1,0:T(8,128)S(1)} %get-tuple-element.635, f32[8,512]{1,0:T(8,128)S(1)} %get-tuple-element.636, bf16[1024,8,64]{0,2,1:T(8,128)(2,1)S(1)} %get-tuple-element.715, ...), kind=kOutput, calls=%fused_computation.23.clone.1 | convolution fusion | flops 562032640 | bytes 35700740 | tf_op jit(solution)/shard_map/while/body/eval_jaxpr/qhd,khd->hqk/dot_general | solution.py:69
  356.6 11.5 %multiply_convert_fusion.3 = bf16[8,512,1024]{2,1,0:T(8,128)(2,1)S(1)} fusion(f32[8,512,1024]{2,1,0:T(8,128)} %get-tuple-element.637, f32[8,512,1024]{2,1,0:T(8,128)} %fusion.177, f32[8,512]{1,0:T(8,128)S(1)} %get-tuple-element.638), kind=kLoop, calls=%fused_computation.22.clone.1 | loop fusion | flops 12582912 | bytes 41959424 | tf_op jit(solution)/shard_map/while/body/eval_jaxpr/convert_element_type | solution.py:159
  368.1 7.8 bitcast_add_fusion.5
  381.0 9.7 %fusion.177 = f32[8,512,1024]{2,1,0:T(8,128)} fusion(bf16[1024,8,64]{0,2,1:T(8,128)(2,1)} %get-tuple-element.720, bf16[2,512,8,64]{1,3,2,0:T(8,128)(2,1)} %get-tuple-element.718, s32[]{:T(128)S(6)} %copy.123, bf16[512]{0:T(512)(128)(2,1)S(1)} %convert_reduce_fusion.3), kind=kOutput, calls=%fused_computation.38.clone.1 | convolution fusion | flops 537133056 | bytes 18351108 | tf_op jit(solution)/shard_map/while/body/eval_jaxpr/qhd,khd->hqk/dot_general | solution.py:155
  390.6 14.8 %multiply_reduce_fusion.4 = (f32[8,512]{1,0:T(8,128)S(1)}, f32[8,512,1024]{2,1,0:T(8,128)}) fusion(f32[8,512,1024]{2,1,0:T(8,128)} %fusion.177, f32[8,512]{1,0:T(8,128)S(1)} %get-tuple-element.635, f32[8,512]{1,0:T(8,128)S(1)} %get-tuple-element.636, bf16[1024,8,64]{0,2,1:T(8,128)(2,1)S(1)} %get-tuple-element.715, ...), kind=kOutput, calls=%fused_computation.23.clone.1 | convolution fusion | flops 562032640 | bytes 35700740 | tf_op jit(solution)/shard_map/while/body/eval_jaxpr/qhd,khd->hqk/dot_general | solution.py:69
  405.5 11.5 %multiply_convert_fusion.3 = bf16[8,512,1024]{2,1,0:T(8,128)(2,1)S(1)} fusion(f32[8,512,1024]{2,1,0:T(8,128)} %get-tuple-element.637, f32[8,512,1024]{2,1,0:T(8,128)} %fusion.177, f32[8,512]{1,0:T(8,128)S(1)} %get-tuple-element.638), kind=kLoop, calls=%fused_computation.22.clone.1 | loop fusion | flops 12582912 | bytes 41959424 | tf_op jit(solution)/shard_map/while/body/eval_jaxpr/convert_element_type | solution.py:159
  417.0 7.8 bitcast_add_fusion.5
  437.0 7.8 copy.89
  444.8 5.7 all-to-all-start.3
  462.1 36.0 %all-to-all-done.3 = bf16[1024,3,512]{2,1,0:T(4,128)(2,1)} async-done(((bf16[1024,3,512]{2,1,0:T(4,128)(2,1)}), bf16[1024,3,512]{2,1,0:T(4,128)(2,1)}, u32[]{:S(2)}, u32[]{:S(2)}) %all-to-all-start.3) | async-done | bytes 3145760 | tf_op jit(solution)/shard_map/all_to_all | solution.py:300
  502.7 4.8 copy.91
  514.3 167.8 %all-reduce.12.cloned.1.call-done = (f32[1024,128]{1,0:T(8,128)}, f32[128,3072]{1,0:T(8,128)}, f32[1024,128]{1,0:T(8,128)}, f32[128,1024]{1,0:T(8,128)}, f32[102...) async-done(((f32[1024,128]{1,0:T(8,128)}, f32[128,3072]{1,0:T(8,128)}, f32[1024,128]{1,0:T(8,128)}, f32[128,1024]{1,0:T(8,128)}, ...) | async-done | bytes 8388624 | tf_op jit(solution)/shard_map/psum | solution.py:307
  682.7 8.6 fusion.72
  693.6 5.7 fusion.75
  703.1 179.8 %all-reduce.14.cloned.1.call-done = (f32[1024,128]{1,0:T(8,128)}, f32[128,3072]{1,0:T(8,128)}, f32[1024,128]{1,0:T(8,128)}, f32[128,1024]{1,0:T(8,128)}, f32[102...) async-done(((f32[1024,128]{1,0:T(8,128)}, f32[128,3072]{1,0:T(8,128)}, f32[1024,128]{1,0:T(8,128)}, f32[128,1024]{1,0:T(8,128)}, ...) | async-done | bytes 8388624 | tf_op jit(solution)/shard_map/psum | solution.py:320
  (340 shorter events, 161.2 us)
Async XLA Ops:
  7.2 245.5 %copy-start = (bf16[128,4096]{1,0:T(8,128)(2,1)S(1)}, bf16[128,4096]{1,0:T(8,128)(2,1)}, u32[]{:S(2)}) copy-start(bf16[128,4096]{1,0:T(8,128)(2,1)} %param.49) | copy-start | bytes 3145732
  7.2 81.1 %copy-start.55 = (bf16[1024,128]{1,0:T(8,128)(2,1)S(1)}, bf16[1024,128]{1,0:T(8,128)(2,1)}, u32[]{:S(2)}) copy-start(bf16[1024,128]{1,0:T(8,128)(2,1)} %param.44) | copy-start | bytes 786436
  7.2 81.6 %all-gather.6.cloned.1.call-start = ((), (), s32[]{:S(2)}) async-start(), calls=%async_computation.4 | async-start | bytes 6684672 | tf_op jit(solution)/shard_map/all_gather | solution.py:240
  7.9 228.9 %all-gather.8.cloned.1.call-start = ((), (), s32[]{:S(2)}) async-start(), calls=%async_computation.5 | async-start | bytes 2228224 | tf_op jit(solution)/shard_map/all_gather | solution.py:241
  8.7 236.2 %all-gather.10.cloned.1.call-start = ((), (), s32[]{:S(2)}) async-start(), calls=%async_computation.6 | async-start | bytes 8912896 | tf_op jit(solution)/shard_map/all_gather | solution.py:257
  108.3 49.2 %all-to-all-start = ((bf16[512,3,1024]{0,1,2:T(4,128)(2,1)}), bf16[512,3,1024]{0,1,2:T(4,128)(2,1)}, u32[]{:S(2)}, u32[]{:S(2)}) async-start(bf16[512,3,1024]{0,1,2:T(4,128)(2,1)} %copy.78), calls=%async_computation | async-start | bytes 8388608 | tf_op jit(solution)/shard_map/all_to_all | solution.py:249
  114.1 159.8 %all-gather.12.cloned.1.call-start = ((), (), s32[]{:S(2)}) async-start(), calls=%async_computation.7 | async-start | bytes 8912896 | tf_op jit(solution)/shard_map/all_gather | solution.py:259
  179.6 34.9 %copy-start.82 = (bf16[256]{0:T(256)(128)(2,1)S(1)}, bf16[256]{0:T(256)(128)(2,1)}, u32[]{:S(2)}) copy-start(bf16[256]{0:T(256)(128)(2,1)} %param.41) | copy-start | bytes 1540
  179.6 34.9 %copy-start.74 = (bf16[1024]{0:T(1024)(128)(2,1)S(1)}, bf16[1024]{0:T(1024)(128)(2,1)}, u32[]{:S(2)}) copy-start(bf16[1024]{0:T(1024)(128)(2,1)} %get-tuple-element.447) | copy-start | bytes 6148
  179.6 34.9 %copy-start.73 = (bf16[1024]{0:T(1024)(128)(2,1)S(1)}, bf16[1024]{0:T(1024)(128)(2,1)}, u32[]{:S(2)}) copy-start(bf16[1024]{0:T(1024)(128)(2,1)} %get-tuple-element.445) | copy-start | bytes 6148
  179.6 34.9 %copy-start.72 = (bf16[1024]{0:T(1024)(128)(2,1)S(1)}, bf16[1024]{0:T(1024)(128)(2,1)}, u32[]{:S(2)}) copy-start(bf16[1024]{0:T(1024)(128)(2,1)} %get-tuple-element.446) | copy-start | bytes 6148
  179.6 53.1 %copy-start.53 = (bf16[128,1024]{1,0:T(8,128)(2,1)S(1)}, bf16[128,1024]{1,0:T(8,128)(2,1)}, u32[]{:S(2)}) copy-start(bf16[128,1024]{1,0:T(8,128)(2,1)} %param.51) | copy-start | bytes 786436
  179.6 53.1 %copy-start.76 = (s32[512]{0:T(512)S(1)}, s32[512]{0:T(512)}, u32[]{:S(2)}) copy-start(s32[512]{0:T(512)} %copy-done.75) | copy-start | bytes 6148
  179.6 53.1 %copy-start.79 = (pred[512]{0:T(512)(128)(4,1)S(1)}, pred[512]{0:T(512)(128)(4,1)}, u32[]{:S(2)}) copy-start(pred[512]{0:T(512)(128)(4,1)} %copy-done.78) | copy-start | bytes 1540
  179.6 53.1 %copy-start.84 = (s32[128]{0:T(128)S(1)}, s32[128]{0:T(128)}, u32[]{:S(2)}) copy-start(s32[128]{0:T(128)} %copy-done.83) | copy-start | bytes 1540
  210.0 25.0 %all-to-all-start.1 = ((bf16[2,512,512]{1,2,0:T(8,128)(2,1)}), bf16[2,512,512]{1,2,0:T(8,128)(2,1)}, u32[]{:S(2)}, u32[]{:S(2)}) async-start(bf16[2,512,512]{1,2,0:T(8,128)(2,1)} %bitcast.244), calls=%async_computation.1 | async-start | bytes 2097152 | tf_op jit(solution)/shard_map/all_to_all | solution.py:251
  273.8 11.7 %copy-start.59 = (bf16[512,128]{1,0:T(8,128)(2,1)S(1)}, bf16[512,128]{1,0:T(8,128)(2,1)}, u32[]{:S(2)}) copy-start(bf16[512,128]{1,0:T(8,128)(2,1)} %fusion.53) | copy-start | bytes 393220
  273.8 11.7 %copy-start.81 = (bf16[4096,128]{1,0:T(8,128)(2,1)S(1)}, bf16[4096,128]{1,0:T(8,128)(2,1)}, u32[]{:S(2)}) copy-start(bf16[4096,128]{1,0:T(8,128)(2,1)} %param.50) | copy-start | bytes 3145732
  273.8 24.4 %slice-start = ((s8[8388608]{0:T(1024)(128)(4,1)}), s8[4194304]{0:T(1024)(128)(4,1)S(1)}, s32[]{:S(2)}) async-start(s8[8388608]{0:T(1024)(128)(4,1)} %bitcast.251), calls=%async_computation.10 | async-start | bytes 8388608
  285.6 12.7 %slice-start.1 = ((s8[8388608]{0:T(1024)(128)(4,1)}), s8[4194304]{0:T(1024)(128)(4,1)S(1)}, s32[]{:S(2)}) async-start(s8[8388608]{0:T(1024)(128)(4,1)} %bitcast.251), calls=%async_computation.11 | async-start | bytes 8388608
  310.0 21.6 %copy-start.3 = (bf16[1024,8,64]{0,2,1:T(8,128)(2,1)S(1)}, bf16[1024,8,64]{0,2,1:T(8,128)(2,1)}, u32[]{:S(2)}) copy-start(bf16[1024,8,64]{0,2,1:T(8,128)(2,1)} %copy-done.2) | copy-start | bytes 3145732
  310.0 19.2 %all-to-all-start.2 = ((bf16[512,2,512]{2,0,1:T(8,128)(2,1)}), bf16[512,2,512]{2,0,1:T(8,128)(2,1)}, u32[]{:S(2)}, u32[]{:S(2)}) async-start(bf16[512,2,512]{2,0,1:T(8,128)(2,1)} %bitcast.241), calls=%async_computation.2 | async-start | bytes 2097152 | tf_op jit(solution)/shard_map/all_to_all | solution.py:294
  332.1 9.7 %copy-start.14 = (bf16[2,512,8,64]{1,3,2,0:T(8,128)(2,1)S(1)}, bf16[2,512,8,64]{1,3,2,0:T(8,128)(2,1)}, u32[]{:S(2)}) copy-start(bf16[2,512,8,64]{1,3,2,0:T(8,128)(2,1)} %get-tuple-element.711) | copy-start | bytes 3145732 | tf_op jit(solution)/shard_map/while
  356.6 11.5 %copy-start.8 = (f32[1024,8,64]{0,2,1:T(8,128)S(1)}, f32[1024,8,64]{0,2,1:T(8,128)}, u32[]{:S(2)}) copy-start(f32[1024,8,64]{0,2,1:T(8,128)} %get-tuple-element.693) | copy-start | bytes 6291460 | tf_op jit(solution)/shard_map/while
  356.6 11.5 %copy-start.13 = (bf16[2,512,8,64]{1,3,2,0:T(8,128)(2,1)S(1)}, bf16[2,512,8,64]{1,3,2,0:T(8,128)(2,1)}, u32[]{:S(2)}) copy-start(bf16[2,512,8,64]{1,3,2,0:T(8,128)(2,1)} %get-tuple-element.718) | copy-start | bytes 3145732 | tf_op jit(solution)/shard_map/while
  380.9 9.7 %copy-start.14 = (bf16[2,512,8,64]{1,3,2,0:T(8,128)(2,1)S(1)}, bf16[2,512,8,64]{1,3,2,0:T(8,128)(2,1)}, u32[]{:S(2)}) copy-start(bf16[2,512,8,64]{1,3,2,0:T(8,128)(2,1)} %get-tuple-element.711) | copy-start | bytes 3145732 | tf_op jit(solution)/shard_map/while
  405.5 11.5 %copy-start.8 = (f32[1024,8,64]{0,2,1:T(8,128)S(1)}, f32[1024,8,64]{0,2,1:T(8,128)}, u32[]{:S(2)}) copy-start(f32[1024,8,64]{0,2,1:T(8,128)} %get-tuple-element.693) | copy-start | bytes 6291460 | tf_op jit(solution)/shard_map/while
  405.5 11.5 %copy-start.13 = (bf16[2,512,8,64]{1,3,2,0:T(8,128)(2,1)S(1)}, bf16[2,512,8,64]{1,3,2,0:T(8,128)(2,1)}, u32[]{:S(2)}) copy-start(bf16[2,512,8,64]{1,3,2,0:T(8,128)(2,1)} %get-tuple-element.718) | copy-start | bytes 3145732 | tf_op jit(solution)/shard_map/while
  444.8 53.2 %all-to-all-start.3 = ((bf16[1024,3,512]{2,1,0:T(4,128)(2,1)}), bf16[1024,3,512]{2,1,0:T(4,128)(2,1)}, u32[]{:S(2)}, u32[]{:S(2)}) async-start(bf16[1024,3,512]{2,1,0:T(4,128)(2,1)} %copy.89), calls=%async_computation.3 | async-start | bytes 8388608 | tf_op jit(solution)/shard_map/all_to_all | solution.py:300
  450.6 231.4 %all-reduce.12.cloned.1.call-start = ((), (), s32[]{:S(2)}) async-start(), calls=%async_computation.8 | async-start | bytes 16777216 | tf_op jit(solution)/shard_map/psum | solution.py:307
  514.2 368.7 %all-reduce.14.cloned.1.call-start = ((), (), s32[]{:S(2)}) async-start(), calls=%async_computation.9 | async-start | bytes 16777216 | tf_op jit(solution)/shard_map/psum | solution.py:320
  682.7 8.6 copy-start.54
  (74 other events, 305.3 us)
Sparse Core Ops, SparseCore 0:
  10.3 64.6 all-gather.5
  77.2 40.2 all-gather.7
  119.6 73.0 all-gather.9
  194.7 72.9 all-gather.11
  514.3 167.6 all-reduce.11
  684.9 197.9 all-reduce.13
